TPU v7x, 32 devices: a whole 2x2x4 slice. The times are simulated.
32 devices in a mesh: dp: 8 (over z, x), tensor: 4 (over y, core).
Axes of the slice: x: 2, y: 2, z: 4, core: 2. Of those that a mesh axis runs over, the one named last changes fastest.
Arguments:
- hidden: bfloat16 [8192, 2560], P('dp', 'tensor'), may hold values from -6 to 6
- out_grad: bfloat16 [8192, 2560], P('dp', 'tensor'), may hold values from -6 to 6
- memory: bfloat16 [8192, 1280], P('dp'), may hold values from -6 to 6
- w_key: bfloat16 [1280, 2560], P(None, 'tensor'), may hold values from -0.15625 to 0.15625
- w_value: bfloat16 [1280, 2560], P(None, 'tensor'), may hold values from -0.15625 to 0.15625
- row_owner: int32 [8192, 8], P('dp'), may hold values from 0 to 31, all different within a row; in each aligned block of 256 rows (0 to 255, 256 to 511, ...) at most 128 rows name the same one
- row_slot: int32 [8192, 8], P('dp'), may hold values from 0 to 511
- mem_table: float32 [16384, 160], P(('dp', 'tensor')), may hold values from -6 to 6
- adagrad_sum: float32 [16384, 160], P(('dp', 'tensor')), may hold values from 0.05 to 2
Outputs:
- hidden_grad: bfloat16 [8192, 2560], P('dp', 'tensor')
- key_weight_grad: float32 [1280, 2560], P('dp', 'tensor')
- value_weight_grad: float32 [1280, 2560], P('dp', 'tensor')
- new_table: float32 [16384, 160], P(('dp', 'tensor'))
- new_sum: float32 [16384, 160], P(('dp', 'tensor'))
Inputs may be any that keep to these rules, and one draw needn't show every extreme that they name: `row_owner`: each token's 8 owners are distinct. Within a dp shard, take the tokens in order in aligned blocks of 256: in each block no owner is named more than 128 times, a bound that some owner reaches in some or all blocks. `row_slot`: A few row indices are retrieved very often.
All inputs are finite; a program needn't handle non-finite values.
Results may differ from a plain program's by a relative error of at most 0.0034.
Values sent between devices are 32-bit elements; how exact they have to be, the bound alone decides.
A program may use at most 128 MiB of HBM per device.

v0:
```python
import math

import jax
import jax.numpy as jnp
from jax import lax
from jax.sharding import PartitionSpec as P

D = 2560


LEARN_RATE = 0.5
EPSILON = 1e-06


def body(hidden, out_grad, memory, w_key, w_value, row_owner, row_slot, mem_table, adagrad_sum):
    highest = lax.Precision.HIGHEST
    scale_root = jnp.sqrt(jnp.asarray(D, jnp.float32))
    local_width = w_key.shape[1]
    proj_key = jnp.dot(memory, w_key, preferred_element_type=jnp.float32)
    proj_value = jnp.dot(memory, w_value, preferred_element_type=jnp.float32)
    part_score = jnp.sum(hidden.astype(jnp.float32) * proj_key, axis=1)
    part_gate = jnp.sum(out_grad.astype(jnp.float32) * proj_value, axis=1)
    scores, gate_grad = lax.psum((part_score, part_gate), "tensor")
    gate_value = jax.nn.sigmoid(scores / scale_root)
    score_grad = gate_grad * gate_value * (1.0 - gate_value) / scale_root
    value_grad = (gate_value[:, None] * out_grad.astype(jnp.float32)).astype(jnp.bfloat16)
    key_grad = (score_grad[:, None] * hidden.astype(jnp.float32)).astype(jnp.bfloat16)
    hidden_grad = (score_grad[:, None] * proj_key).astype(jnp.bfloat16)
    joined = jnp.concatenate([key_grad, value_grad], axis=1)
    over_tokens = (((0,), (0,)), ((), ()))
    both_grads = lax.psum_scatter(
        lax.dot_general(memory, joined, over_tokens, preferred_element_type=jnp.float32),
        "dp",
        scatter_dimension=0,
        tiled=True,
    )
    key_weight_grad = both_grads[:, :local_width]
    value_weight_grad = both_grads[:, local_width:]
    over_features = (((1,), (1,)), ((), ()))
    tensor_count = lax.axis_size("tensor")
    quarter = memory.shape[0] // tensor_count
    total = lax.dot_general(value_grad, w_value, over_features, preferred_element_type=jnp.float32)
    memory_grad = lax.psum_scatter(
        total + lax.dot_general(key_grad, w_key, over_features, preferred_element_type=jnp.float32),
        "tensor",
        scatter_dimension=0,
        tiled=True,
    )
    heads = row_owner.shape[1]
    row_width = memory_grad.shape[1] // heads
    first_row = lax.axis_index("tensor") * quarter
    owners = lax.dynamic_slice_in_dim(row_owner, first_row, quarter, 0)
    slots = lax.dynamic_slice_in_dim(row_slot, first_row, quarter, 0)
    grads = memory_grad.reshape(-1, row_width)
    dp_count = lax.axis_size("dp")
    owner_count = dp_count * tensor_count
    capacity = max(2, 2 * quarter * heads // owner_count)
    owner_ids = jnp.arange(owner_count, dtype=jnp.int32)
    matches = (owners[:, :, None] == owner_ids[None, None, :]).astype(jnp.float32)
    token_hits = jnp.sum(matches, axis=1)
    token_ids = jnp.arange(quarter, dtype=jnp.int32)
    earlier = (token_ids[:, None] > token_ids[None, :]).astype(jnp.float32)
    before = jnp.dot(earlier, token_hits, precision=highest, preferred_element_type=jnp.float32)
    ranks = jnp.sum(matches * before[:, None, :], axis=2).astype(jnp.int32)
    placed = (owners * capacity + ranks).reshape(-1)
    slot_plus = (slots.reshape(-1) + 1).astype(jnp.float32)
    total_slots = owner_count * capacity
    pack_block = math.gcd(total_slots, 512)
    pack_starts = jnp.arange(total_slots // pack_block, dtype=jnp.int32) * pack_block
    block_ids = jnp.arange(pack_block, dtype=jnp.int32)

    def pack_block_fn(first):
        select = (placed[:, None] == first + block_ids[None, :]).astype(jnp.float32)
        block_grads = lax.dot_general(
            select, grads, over_tokens, precision=highest, preferred_element_type=jnp.float32
        )
        block_slots = jnp.dot(
            slot_plus, select, precision=highest, preferred_element_type=jnp.float32
        )
        return (block_grads, block_slots)

    packed_grads, packed_slots = lax.map(pack_block_fn, pack_starts)
    send_grads = packed_grads.reshape(total_slots, row_width)
    send_slots = packed_slots.reshape(total_slots).astype(jnp.int32) - 1
    sectioned_grads = send_grads.reshape(dp_count, tensor_count, capacity, row_width)
    sectioned_slots = send_slots.reshape(dp_count, tensor_count, capacity)
    recv_grads, recv_slots = (
        lax.all_to_all(
            lax.all_to_all(sectioned_grads, "dp", split_axis=0, concat_axis=0, tiled=True),
            "tensor",
            split_axis=1,
            concat_axis=1,
            tiled=True,
        ),
        lax.all_to_all(
            lax.all_to_all(sectioned_slots, "dp", split_axis=0, concat_axis=0, tiled=True),
            "tensor",
            split_axis=1,
            concat_axis=1,
            tiled=True,
        ),
    )
    recv_grads = recv_grads.reshape(-1, row_width)
    recv_slots = recv_slots.reshape(-1)
    table_rows = mem_table.shape[0]
    sum_block = math.gcd(table_rows, 512)
    sum_starts = jnp.arange(table_rows // sum_block, dtype=jnp.int32) * sum_block
    row_ids = jnp.arange(sum_block, dtype=jnp.int32)

    def sum_block_fn(first):
        select = (recv_slots[:, None] == first + row_ids[None, :]).astype(jnp.float32)
        return lax.dot_general(
            select, recv_grads, over_tokens, precision=highest, preferred_element_type=jnp.float32
        )

    row_sum = lax.map(sum_block_fn, sum_starts).reshape(table_rows, row_width)
    new_sum = adagrad_sum + row_sum * row_sum
    new_table = mem_table - LEARN_RATE * row_sum / (jnp.sqrt(new_sum) + EPSILON)
    return (hidden_grad, key_weight_grad, value_weight_grad, new_table, new_sum)


def solution(mesh):
    return jax.shard_map(
        body,
        mesh=mesh,
        in_specs=(
            P("dp", "tensor"),
            P("dp", "tensor"),
            P("dp", None),
            P(None, "tensor"),
            P(None, "tensor"),
            P("dp", None),
            P("dp", None),
            P(("dp", "tensor"), None),
            P(("dp", "tensor"), None),
        ),
        out_specs=(
            P("dp", "tensor"),
            P("dp", "tensor"),
            P("dp", "tensor"),
            P(("dp", "tensor"), None),
            P(("dp", "tensor"), None),
        ),
        check_vma=False,
    )
```

profile of v0, /device:TPU:0, one launch (start us, length us, event | category | flops | bytes accessed | tf_op | source)
XLA Modules:
  0.0 283.9 jit_solution(9969671385588224455)
XLA Ops:
  7.2 2.6 copy.55
  9.8 2.4 copy.54
  12.3 3.9 %fusion.18 = f32[1024]{0:T(1024)S(1)} fusion(bf16[1024,640]{0,1:T(8,128)(2,1)} %copy.54, bf16[1024,1280]{1,0:T(8,128)(2,1)S(1)} %copy-done, bf16[1280,640]{1,0:T(8,128)(2,1)} %param.15), kind=kOutput, calls=%fused_computation.21 | convolution fusion | flops 1679686656 | bytes 5574656 | tf_op jit(solution)/shard_map/dot_general | solution.py:20
  16.2 3.4 %fusion.20 = (f32[1024]{0:T(1024)S(1)}, f32[1024,640]{0,1:T(8,128)}) fusion(bf16[1024,640]{0,1:T(8,128)(2,1)S(1)} %copy-done.3, bf16[1024,1280]{1,0:T(8,128)(2,1)S(1)} %copy-done, bf16[1280,640]{1,0:T(8,128)(2,1)S(1)} %copy-done.4), kind=kOutput, calls=%fused_computation.23 | convolution fusion | flops 1679686656 | bytes 8196096 | tf_op jit(solution)/shard_map/dot_general | solution.py:19
  19.6 8.5 %all-reduce = (f32[1024]{0:T(1024)S(1)}, f32[1024]{0:T(1024)S(1)}) all-reduce(f32[1024]{0:T(1024)S(1)} %fusion.18, f32[1024]{0:T(1024)S(1)} %get-tuple-element.137), channel_id=1, replica_groups=mesh['dp'=8,'tensor'=4] {'tensor'}, use_global_device_ids=true, to_apply=%region_1.0 | all-reduce | flops 2048 | bytes 16384 | tf_op jit(solution)/shard_map/psum | solution.py:23
  28.2 4.5 %fusion.21 = (bf16[1024,640]{0,1:T(8,128)(2,1)S(1)}, bf16[1024,640]{0,1:T(8,128)(2,1)}, bf16[1024,640]{0,1:T(8,128)(2,1)S(1)}) fusion(bf16[1024,640]{0,1:T(8,128)(2,1)} %copy.55, f32[1024]{0:T(1024)S(1)} %get-tuple-element.136, f32[1024,640]{0,1:T(8,128)} %get-tuple-element.138, bf16[1024,640]{0,1:T(8,128)(2,1)} %copy.54, f32[1024]{0:T(1024)S(1)} %get-tuple-element.135), kind=kLoop, calls=%fused_computation.24 | loop fusion | flops 5242880 | bytes 9183232 | tf_op jit(solution)/shard_map/convert_element_type | solution.py:27
  35.1 4.6 %convolution_add_fusion = f32[1024,1280]{1,0:T(8,128)} fusion(f32[1024,1280]{1,0:T(8,128)S(1)} %fusion.28, bf16[1024,640]{0,1:T(8,128)(2,1)S(1)} %get-tuple-element.133, bf16[1280,640]{1,0:T(8,128)(2,1)S(1)} %copy-done.5), kind=kOutput, calls=%fused_computation.15 | convolution fusion | flops 1679032320 | bytes 13434880 | tf_op jit(solution)/shard_map/dot_general | solution.py:44
  39.9 8.0 %convolution_bitcast_fusion = f32[1280,1280]{0,1:T(8,128)} fusion(bf16[1024,1280]{1,0:T(8,128)(2,1)S(1)} %copy-done, bf16[1024,640]{0,1:T(8,128)(2,1)} %copy-done.6, bf16[1024,640]{0,1:T(8,128)(2,1)} %copy-done.2), kind=kOutput, calls=%fused_computation.12 | convolution fusion | flops 3360686080 | bytes 11796480 | tf_op jit(solution)/shard_map/dot_general | solution.py:32
  47.9 8.4 %copy.65 = f32[1280,1280]{1,0:T(8,128)} copy(f32[1280,1280]{0,1:T(8,128)} %convolution_bitcast_fusion) | data formatting | bytes 13107200
  58.0 33.5 %reduce-scatter.5.cloned.1.call-done = f32[256,1280]{1,0:T(8,128)} async-done(((f32[1024,1280]{1,0:T(8,128)}), f32[256,1280]{1,0:T(8,128)}) %reduce-scatter.5.cloned.1.call-update) | async-done | bytes 1310736 | tf_op jit(solution)/shard_map/reduce_scatter | solution.py:43
  93.9 46.9 %while.18 = (s32[]{:T(128)}, f32[8,512,160]{1,2,0:T(8,128)}, f32[8,512]{1,0:T(8,128)S(1)}, s32[256,8]{1,0:T(8,128)}, s32[8]{0:T(128)S(1)}, /*index=5*/f32[2048,1...) while((s32[]{:T(128)}, f32[8,512,160]{1,2,0:T(8,128)}, ...), condition=%wide.wide.region_9.10_spmd.clone, body=%wide.wide.region_8.9_spmd.clone.sunk | while | flops 2027946496 | bytes 1675397 | solution.py:82
  96.5 3.2 %fusion.58 = f32[8,512,160]{1,2,0:T(8,128)} fusion(f32[8,512,160]{1,2,0:T(8,128)} %get-tuple-element.230, s32[]{:T(128)S(6)} %copy.74, f32[2048,160]{1,0:T(8,128)S(1)} %get-tuple-element.244, s32[512]{0:T(512)S(1)} %iota_add_fusion.3, s32[2048]{0:T(1024)S(1)} %get-tuple-element.246), kind=kOutput, calls=%fused_computation.10.clone.clone.1 | convolution fusion | flops 2014314496 | bytes 1648644 | tf_op jit(solution)/shard_map/while/body/eval_jaxpr/dot_general | solution.py:74
  102.4 3.2 %fusion.58 = f32[8,512,160]{1,2,0:T(8,128)} fusion(f32[8,512,160]{1,2,0:T(8,128)} %get-tuple-element.230, s32[]{:T(128)S(6)} %copy.74, f32[2048,160]{1,0:T(8,128)S(1)} %get-tuple-element.244, s32[512]{0:T(512)S(1)} %iota_add_fusion.3, s32[2048]{0:T(1024)S(1)} %get-tuple-element.246), kind=kOutput, calls=%fused_computation.10.clone.clone.1 | convolution fusion | flops 2014314496 | bytes 1648644 | tf_op jit(solution)/shard_map/while/body/eval_jaxpr/dot_general | solution.py:74
  108.3 3.2 %fusion.58 = f32[8,512,160]{1,2,0:T(8,128)} fusion(f32[8,512,160]{1,2,0:T(8,128)} %get-tuple-element.230, s32[]{:T(128)S(6)} %copy.74, f32[2048,160]{1,0:T(8,128)S(1)} %get-tuple-element.244, s32[512]{0:T(512)S(1)} %iota_add_fusion.3, s32[2048]{0:T(1024)S(1)} %get-tuple-element.246), kind=kOutput, calls=%fused_computation.10.clone.clone.1 | convolution fusion | flops 2014314496 | bytes 1648644 | tf_op jit(solution)/shard_map/while/body/eval_jaxpr/dot_general | solution.py:74
  114.1 3.2 %fusion.58 = f32[8,512,160]{1,2,0:T(8,128)} fusion(f32[8,512,160]{1,2,0:T(8,128)} %get-tuple-element.230, s32[]{:T(128)S(6)} %copy.74, f32[2048,160]{1,0:T(8,128)S(1)} %get-tuple-element.244, s32[512]{0:T(512)S(1)} %iota_add_fusion.3, s32[2048]{0:T(1024)S(1)} %get-tuple-element.246), kind=kOutput, calls=%fused_computation.10.clone.clone.1 | convolution fusion | flops 2014314496 | bytes 1648644 | tf_op jit(solution)/shard_map/while/body/eval_jaxpr/dot_general | solution.py:74
  119.9 3.2 %fusion.58 = f32[8,512,160]{1,2,0:T(8,128)} fusion(f32[8,512,160]{1,2,0:T(8,128)} %get-tuple-element.230, s32[]{:T(128)S(6)} %copy.74, f32[2048,160]{1,0:T(8,128)S(1)} %get-tuple-element.244, s32[512]{0:T(512)S(1)} %iota_add_fusion.3, s32[2048]{0:T(1024)S(1)} %get-tuple-element.246), kind=kOutput, calls=%fused_computation.10.clone.clone.1 | convolution fusion | flops 2014314496 | bytes 1648644 | tf_op jit(solution)/shard_map/while/body/eval_jaxpr/dot_general | solution.py:74
  125.8 3.2 %fusion.58 = f32[8,512,160]{1,2,0:T(8,128)} fusion(f32[8,512,160]{1,2,0:T(8,128)} %get-tuple-element.230, s32[]{:T(128)S(6)} %copy.74, f32[2048,160]{1,0:T(8,128)S(1)} %get-tuple-element.244, s32[512]{0:T(512)S(1)} %iota_add_fusion.3, s32[2048]{0:T(1024)S(1)} %get-tuple-element.246), kind=kOutput, calls=%fused_computation.10.clone.clone.1 | convolution fusion | flops 2014314496 | bytes 1648644 | tf_op jit(solution)/shard_map/while/body/eval_jaxpr/dot_general | solution.py:74
  131.7 3.2 %fusion.58 = f32[8,512,160]{1,2,0:T(8,128)} fusion(f32[8,512,160]{1,2,0:T(8,128)} %get-tuple-element.230, s32[]{:T(128)S(6)} %copy.74, f32[2048,160]{1,0:T(8,128)S(1)} %get-tuple-element.244, s32[512]{0:T(512)S(1)} %iota_add_fusion.3, s32[2048]{0:T(1024)S(1)} %get-tuple-element.246), kind=kOutput, calls=%fused_computation.10.clone.clone.1 | convolution fusion | flops 2014314496 | bytes 1648644 | tf_op jit(solution)/shard_map/while/body/eval_jaxpr/dot_general | solution.py:74
  137.6 3.3 %fusion.58 = f32[8,512,160]{1,2,0:T(8,128)} fusion(f32[8,512,160]{1,2,0:T(8,128)} %get-tuple-element.230, s32[]{:T(128)S(6)} %copy.74, f32[2048,160]{1,0:T(8,128)S(1)} %get-tuple-element.244, s32[512]{0:T(512)S(1)} %iota_add_fusion.3, s32[2048]{0:T(1024)S(1)} %get-tuple-element.246), kind=kOutput, calls=%fused_computation.10.clone.clone.1 | convolution fusion | flops 2014314496 | bytes 1648644 | tf_op jit(solution)/shard_map/while/body/eval_jaxpr/dot_general | solution.py:74
  141.4 5.5 %all-to-all-start = ((s32[8,4,128]{2,1,0:T(4,128)}), s32[8,4,128]{2,1,0:T(4,128)S(1)}, u32[]{:S(2)}, u32[]{:S(2)}) async-start(s32[8,4,128]{2,1,0:T(4,128)} %sub.14), calls=%async_computation.1 | async-start | bytes 32768 | tf_op jit(solution)/shard_map/all_to_all | solution.py:96
  147.0 4.0 %reshape_reshape.3 = f32[8,4,128,160]{2,1,3,0:T(4,128)} reshape(f32[8,512,160]{1,2,0:T(8,128)} %get-tuple-element.64) | data formatting | bytes 5242880 | tf_op jit(solution)/shard_map/reshape;reshape | solution.py:85
  150.9 3.0 %all-to-all-done = s32[8,4,128]{2,1,0:T(4,128)S(1)} async-done(((s32[8,4,128]{2,1,0:T(4,128)}), s32[8,4,128]{2,1,0:T(4,128)S(1)}, u32[]{:S(2)}, u32[]{:S(2)}) %all-to-all-start) | async-done | bytes 16416 | tf_op jit(solution)/shard_map/all_to_all | solution.py:96
  153.9 3.6 %all-to-all-start.2 = ((f32[8,4,128,160]{2,1,3,0:T(4,128)}), f32[8,4,128,160]{2,1,3,0:T(4,128)S(1)}, u32[]{:S(2)}, u32[]{:S(2)}) async-start(f32[8,4,128,160]{2,1,3,0:T(4,128)} %reshape_reshape.3), calls=%async_computation.3 | async-start | bytes 5242880 | tf_op jit(solution)/shard_map/all_to_all | solution.py:89
  158.2 63.3 %all-to-all-done.2 = f32[8,4,128,160]{2,1,3,0:T(4,128)S(1)} async-done(((f32[8,4,128,160]{2,1,3,0:T(4,128)}), f32[8,4,128,160]{2,1,3,0:T(4,128)S(1)}, u32[]{:S(2)}, u32[]{:S(2)}) %all-to-all-start.2) | async-done | bytes 2621472 | tf_op jit(solution)/shard_map/all_to_all | solution.py:89
  221.5 3.3 %all-to-all-start.1 = ((s32[8,4,128]{2,0,1:T(8,128)}), s32[8,4,128]{2,0,1:T(8,128)S(1)}, u32[]{:S(2)}, u32[]{:S(2)}) async-start(s32[8,4,128]{2,0,1:T(8,128)} %copy.58), calls=%async_computation.2 | async-start | bytes 32768 | tf_op jit(solution)/shard_map/all_to_all | solution.py:95
  224.7 3.0 %copy.60 = f32[8,4,128,160]{2,0,3,1:T(8,128)} copy(f32[8,4,128,160]{2,1,3,0:T(4,128)S(1)} %all-to-all-done.2) | data formatting | bytes 5242880 | tf_op jit(solution)/shard_map/all_to_all | solution.py:89
  228.5 3.9 %all-to-all-start.3 = ((f32[8,4,128,160]{2,0,3,1:T(8,128)}), f32[8,4,128,160]{2,0,3,1:T(8,128)S(1)}, u32[]{:S(2)}, u32[]{:S(2)}) async-start(f32[8,4,128,160]{2,0,3,1:T(8,128)} %copy.60), calls=%async_computation.4 | async-start | bytes 5242880 | tf_op jit(solution)/shard_map/all_to_all | solution.py:88
  234.9 8.5 %reduce-scatter.7.cloned.1.call-done = f32[160,1280]{1,0:T(8,128)} async-done(((f32[1280,1280]{1,0:T(8,128)}), f32[160,1280]{1,0:T(8,128)}) %reduce-scatter.7.cloned.1.call-update) | async-done | bytes 819216
  245.4 18.1 %all-to-all-done.3 = f32[8,4,128,160]{2,0,3,1:T(8,128)S(1)} async-done(((f32[8,4,128,160]{2,0,3,1:T(8,128)}), f32[8,4,128,160]{2,0,3,1:T(8,128)S(1)}, u32[]{:S(2)}, u32[]{:S(2)}) %all-to-all-start.3) | async-done | bytes 2621472 | tf_op jit(solution)/shard_map/all_to_all | solution.py:88
  263.5 3.2 %copy.61 = f32[8,4,128,160]{2,1,0,3:T(4,128)} copy(f32[8,4,128,160]{2,0,3,1:T(8,128)S(1)} %all-to-all-done.3) | data formatting | bytes 5242880 | tf_op jit(solution)/shard_map/all_to_all | solution.py:88
  266.7 4.2 %reshape.41 = f32[4096,160]{0,1:T(8,128)} reshape(f32[8,4,128,160]{2,1,0,3:T(4,128)} %copy.61) | data formatting | bytes 5242880 | tf_op jit(solution)/shard_map/reshape | solution.py:103
  270.9 6.3 %divide_subtract_fusion = (f32[512,160]{0,1:T(8,128)}, f32[512,160]{0,1:T(8,128)}) fusion(f32[512,160]{0,1:T(8,128)S(1)} %copy-done.9, f32[512,160]{0,1:T(8,128)S(1)} %copy-done.10, f32[4096,160]{0,1:T(8,128)} %reshape.41, s32[4096]{0:T(1024)S(1)} %bitcast.43), kind=kOutput, calls=%fused_computation.29 | convolution fusion | flops 4029120512 | bytes 3948544 | tf_op jit(solution)/shard_map/while/body/eval_jaxpr/dot_general | solution.py:112
  (80 shorter events, 34.0 us)
Async XLA Ops:
  7.2 5.1 %copy-start = (bf16[1024,1280]{1,0:T(8,128)(2,1)S(1)}, bf16[1024,1280]{1,0:T(8,128)(2,1)}, u32[]{:S(2)}) copy-start(bf16[1024,1280]{1,0:T(8,128)(2,1)} %param.13) | copy-start | bytes 7864324
  7.2 84.3 %reduce-scatter.5.cloned.1.call-start = ((), (), s32[]{:S(2)}) async-start(), calls=%async_computation.6 | async-start | bytes 6553600 | tf_op jit(solution)/shard_map/reduce_scatter | solution.py:43
  12.3 3.9 %copy-start.3 = (bf16[1024,640]{0,1:T(8,128)(2,1)S(1)}, bf16[1024,640]{0,1:T(8,128)(2,1)}, u32[]{:S(2)}) copy-start(bf16[1024,640]{0,1:T(8,128)(2,1)} %copy.55) | copy-start | bytes 3932164
  12.3 3.9 %copy-start.4 = (bf16[1280,640]{1,0:T(8,128)(2,1)S(1)}, bf16[1280,640]{1,0:T(8,128)(2,1)}, u32[]{:S(2)}) copy-start(bf16[1280,640]{1,0:T(8,128)(2,1)} %param.14) | copy-start | bytes 4915204
  28.2 4.6 %copy-start.8 = (bf16[1280,640]{1,0:T(8,128)(2,1)S(1)}, bf16[1280,640]{1,0:T(8,128)(2,1)}, u32[]{:S(2)}) copy-start(bf16[1280,640]{1,0:T(8,128)(2,1)} %param.15) | copy-start | bytes 4915204
  32.7 2.3 copy-start.6
  32.7 2.3 copy-start.2
  32.7 2.4 copy-start.5
  39.7 203.6 %reduce-scatter.7.cloned.1.call-start = ((), (), s32[]{:S(2)}) async-start(), calls=%async_computation.7 | async-start | bytes 7372800
  57.6 36.3 %copy-start.7 = (s32[256,8]{1,0:T(8,128)}, s32[256,8]{1,0:T(8,128)S(1)}, u32[]{:S(2)}) copy-start(s32[256,8]{1,0:T(8,128)S(1)} %copy.57) | copy-start | bytes 24580
  141.4 12.5 %all-to-all-start = ((s32[8,4,128]{2,1,0:T(4,128)}), s32[8,4,128]{2,1,0:T(4,128)S(1)}, u32[]{:S(2)}, u32[]{:S(2)}) async-start(s32[8,4,128]{2,1,0:T(4,128)} %sub.14), calls=%async_computation.1 | async-start | bytes 32768 | tf_op jit(solution)/shard_map/all_to_all | solution.py:96
  153.9 67.5 %all-to-all-start.2 = ((f32[8,4,128,160]{2,1,3,0:T(4,128)}), f32[8,4,128,160]{2,1,3,0:T(4,128)S(1)}, u32[]{:S(2)}, u32[]{:S(2)}) async-start(f32[8,4,128,160]{2,1,3,0:T(4,128)} %reshape_reshape.3), calls=%async_computation.3 | async-start | bytes 5242880 | tf_op jit(solution)/shard_map/all_to_all | solution.py:89
  221.5 7.1 %all-to-all-start.1 = ((s32[8,4,128]{2,0,1:T(8,128)}), s32[8,4,128]{2,0,1:T(8,128)S(1)}, u32[]{:S(2)}, u32[]{:S(2)}) async-start(s32[8,4,128]{2,0,1:T(8,128)} %copy.58), calls=%async_computation.2 | async-start | bytes 32768 | tf_op jit(solution)/shard_map/all_to_all | solution.py:95
  228.5 34.9 %all-to-all-start.3 = ((f32[8,4,128,160]{2,0,3,1:T(8,128)}), f32[8,4,128,160]{2,0,3,1:T(8,128)S(1)}, u32[]{:S(2)}, u32[]{:S(2)}) async-start(f32[8,4,128,160]{2,0,3,1:T(8,128)} %copy.60), calls=%async_computation.4 | async-start | bytes 5242880 | tf_op jit(solution)/shard_map/all_to_all | solution.py:88
  266.7 4.2 %copy-start.9 = (f32[512,160]{0,1:T(8,128)S(1)}, f32[512,160]{0,1:T(8,128)}, u32[]{:S(2)}) copy-start(f32[512,160]{0,1:T(8,128)} %param.18) | copy-start | bytes 983044
  266.7 4.2 %copy-start.10 = (f32[512,160]{0,1:T(8,128)S(1)}, f32[512,160]{0,1:T(8,128)}, u32[]{:S(2)}) copy-start(f32[512,160]{0,1:T(8,128)} %param.19) | copy-start | bytes 983044
  270.8 6.3 %copy-start.1 = (bf16[1024,1280]{1,0:T(8,128)(2,1)S(1)}, bf16[1024,1280]{1,0:T(8,128)(2,1)}, u32[]{:S(2)}) copy-start(bf16[1024,1280]{1,0:T(8,128)(2,1)} %param.13) | copy-start | bytes 7864324
Sparse Core Ops, SparseCore 0:
  39.8 51.6 reduce-scatter.4
  95.1 148.1 reduce-scatter.6
where the time goes:
time: 285 us; the launch traced here: 284 us
  waiting for transfers between devices  127 us (45%)
  matrix products  65.3 us (23%)
  local copies, waits for them, and re-layouts  41.5 us (15%)
  starting transfers between devices  16.6 us (6%)
  between operations  14.3 us (5%)
  other arithmetic  10.6 us (4%)
  blocking collectives  8.52 us (3%)
    all_to_all x1, waiting for transfers between devices, body(): lax.all_to_all(sectioned_grads, 'dp', split_axis=0, concat_axis=0, tiled=...  63.3 us
    reduce_scatter x1, waiting for transfers between devices, body(): lax.psum_scatter(total + lax.dot_general(key_grad, w_key, over_features,...  33.5 us
    dot_general x8, matrix products, pack_block_fn(): lax.dot_general(select, grads, over_tokens, precision=highest, preferred_...  25.9 us
    all_to_all x1, waiting for transfers between devices, body(): lax.all_to_all(lax.all_to_all(sectioned_grads, 'dp', split_axis=0, concat...  18.1 us
    unnamed x27, local copies, waits for them, and re-layouts  16.1 us
    dot_general x8, matrix products, pack_block_fn(): jnp.dot(slot_plus, select, precision=highest, preferred_element_type=jnp....  10.7 us
    psum x1, blocking collectives, body(): scores, gate_grad = lax.psum((part_score, part_gate), 'tensor')  8.52 us
    unnamed x3, waiting for transfers between devices  8.49 us
  transfers between devices with their start and end apart: 6, of which 6 were waited for; matrix products, arithmetic and copies ran while one was open for 28% of the time, Pallas kernels for 0%

commit v1 on v0

v1 whole, which is shorter than its diff:
```python
import functools

import jax
import jax.numpy as jnp
from jax import lax
from jax.experimental import pallas as pl
from jax.experimental.pallas import tpu as pltpu
from jax.sharding import PartitionSpec as P

LEARN_RATE = 0.5
EPSILON = 1e-06
MESH = pl.DeviceIdType.MESH
OVER_FEATURES = (((1,), (1,)), ((), ()))


def gate_kernel(count, part_ref, sum_ref, landed, send_sem, recv_sem):
    me = lax.axis_index("tensor")
    dp = lax.axis_index("dp")
    barrier = pltpu.get_barrier_semaphore()
    for k in range(1, count):
        pl.semaphore_signal(
            barrier, inc=1, device_id=(dp, lax.rem(me + k, count)), device_id_type=MESH
        )
    pl.semaphore_wait(barrier, count - 1)
    copies = []
    for k in range(1, count):
        copy = pltpu.make_async_remote_copy(
            src_ref=part_ref,
            dst_ref=landed.at[me],
            send_sem=send_sem.at[k],
            recv_sem=recv_sem.at[k],
            device_id=(dp, lax.rem(me + k, count)),
            device_id_type=MESH,
        )
        copy.start()
        copies.append(copy)
    landed[me] = part_ref[...]
    for copy in copies:
        copy.wait()
    total = landed[0]
    for k in range(1, count):
        total = total + landed[k]
    sum_ref[...] = total


def sum_over_tensor(parts, count):
    return pl.pallas_call(
        functools.partial(gate_kernel, count),
        out_shape=jax.ShapeDtypeStruct(parts.shape, jnp.float32),
        in_specs=[pl.BlockSpec(memory_space=pltpu.VMEM)],
        out_specs=pl.BlockSpec(memory_space=pltpu.VMEM),
        scratch_shapes=[
            pltpu.VMEM((count,) + parts.shape, jnp.float32),
            pltpu.SemaphoreType.DMA((count,)),
            pltpu.SemaphoreType.DMA((count,)),
        ],
        compiler_params=pltpu.CompilerParams(collective_id=0, has_side_effects=True),
        name="gate_sum",
    )(parts)


def exchange_kernel(dp_count, tensor_count, send_ref, recv_ref, local_sem, send_sem, recv_sem):
    count = dp_count * tensor_count
    me = lax.axis_index("dp") * tensor_count + lax.axis_index("tensor")
    barrier = pltpu.get_barrier_semaphore()

    def target(k):
        other = lax.rem(me + k, count)
        return other, (lax.div(other, tensor_count), lax.rem(other, tensor_count))

    def greet(k, carry):
        pl.semaphore_signal(barrier, inc=1, device_id=target(k)[1], device_id_type=MESH)
        return carry

    lax.fori_loop(1, count, greet, 0)
    own = pltpu.make_async_copy(send_ref.at[me], recv_ref.at[me], local_sem)
    own.start()
    pl.semaphore_wait(barrier, count - 1)

    def copy_of(k):
        other, where = target(k)
        return pltpu.make_async_remote_copy(
            src_ref=send_ref.at[other],
            dst_ref=recv_ref.at[me],
            send_sem=send_sem.at[k],
            recv_sem=recv_sem.at[k],
            device_id=where,
            device_id_type=MESH,
        )

    def begin(k, carry):
        copy_of(k).start()
        return carry

    def finish(k, carry):
        copy_of(k).wait()
        return carry

    lax.fori_loop(1, count, begin, 0)
    own.wait()
    lax.fori_loop(1, count, finish, 0)


def exchange_rows(blocks, dp_count, tensor_count):
    count = dp_count * tensor_count
    return pl.pallas_call(
        functools.partial(exchange_kernel, dp_count, tensor_count),
        out_shape=jax.ShapeDtypeStruct(blocks.shape, jnp.float32),
        in_specs=[pl.BlockSpec(memory_space=pl.ANY)],
        out_specs=pl.BlockSpec(memory_space=pl.ANY),
        scratch_shapes=[
            pltpu.SemaphoreType.DMA,
            pltpu.SemaphoreType.DMA((count,)),
            pltpu.SemaphoreType.DMA((count,)),
        ],
        compiler_params=pltpu.CompilerParams(collective_id=1, has_side_effects=True),
        cost_estimate=pl.CostEstimate(
            flops=50_000_000_000, bytes_accessed=2 * blocks.size * 4, transcendentals=0
        ),
        name="exchange_rows",
    )(blocks)


def halves(values):
    high = values.astype(jnp.bfloat16)
    return high, (values - high.astype(jnp.float32)).astype(jnp.bfloat16)


def pack_kernel(width, grads_ref, owners_ref, slots_ref, places_ref, out_ref):
    heads, tokens = owners_ref.shape
    count, capacity = out_ref.shape[0], out_ref.shape[2]
    group = 2

    def step(i, carry):
        for j in range(group):
            dest = i * group + j
            mask = owners_ref[...] == dest
            rows = jnp.zeros((width, tokens), jnp.float32)
            for h in range(heads):
                rows = jnp.where(mask[h : h + 1, :], grads_ref[h * width : (h + 1) * width, :], rows)
            tags = jnp.where(mask, slots_ref[...] + 1.0, 0.0)
            place = places_ref[pl.ds(dest, 1), :]
            spots = lax.broadcasted_iota(jnp.int32, (capacity, tokens), 0)
            choose = (spots == place).astype(jnp.float32).astype(jnp.bfloat16)
            for values, first, last in ((rows, 0, width), (tags, width, width + heads)):
                high, low = halves(values)
                out_ref[dest, first:last, :] = lax.dot_general(
                    high, choose, OVER_FEATURES, preferred_element_type=jnp.float32
                ) + lax.dot_general(low, choose, OVER_FEATURES, preferred_element_type=jnp.float32)
        return carry

    lax.fori_loop(0, count // group, step, 0)


def pack_rows(grads, owners, slots, places, capacity):
    heads, count = owners.shape[0], places.shape[0]
    width = grads.shape[0] // heads
    return pl.pallas_call(
        functools.partial(pack_kernel, width),
        out_shape=jax.ShapeDtypeStruct((count, width + heads, capacity), jnp.float32),
        in_specs=[pl.BlockSpec(memory_space=pltpu.VMEM)] * 4,
        out_specs=pl.BlockSpec(memory_space=pltpu.VMEM),
        cost_estimate=pl.CostEstimate(
            flops=6_000_000_000, bytes_accessed=4_000_000, transcendentals=0
        ),
        name="pack_rows",
    )(grads, owners, slots, places)


def update_kernel(group, recv_ref, table_ref, sums_ref, new_table_ref, new_sums_ref, total):
    rows, width = table_ref.shape
    count, _, capacity = recv_ref.shape
    total[...] = jnp.zeros_like(total)

    def step(i, carry):
        picks, highs, lows = [], [], []
        for j in range(group):
            block = recv_ref[i * group + j]
            tag = jnp.sum(block[width:, :], axis=0, keepdims=True).astype(jnp.int32) - 1
            ids = lax.broadcasted_iota(jnp.int32, (rows, capacity), 0)
            picks.append((ids == tag).astype(jnp.float32).astype(jnp.bfloat16))
            high, low = halves(block[:width, :])
            highs.append(high)
            lows.append(low)
        pick = jnp.concatenate(picks, axis=1) if group > 1 else picks[0]
        high = jnp.concatenate(highs, axis=1) if group > 1 else highs[0]
        low = jnp.concatenate(lows, axis=1) if group > 1 else lows[0]
        total[...] += lax.dot_general(
            pick, high, OVER_FEATURES, preferred_element_type=jnp.float32
        ) + lax.dot_general(pick, low, OVER_FEATURES, preferred_element_type=jnp.float32)
        return carry

    lax.fori_loop(0, count // group, step, 0)
    row_sum = total[...]
    new_sum = sums_ref[...] + row_sum * row_sum
    new_sums_ref[...] = new_sum
    new_table_ref[...] = table_ref[...] - LEARN_RATE * row_sum / (jnp.sqrt(new_sum) + EPSILON)


def update_rows(recv, table, sums):
    group = 4 if recv.shape[2] % 128 == 0 and recv.shape[0] % 4 == 0 else 1
    return pl.pallas_call(
        functools.partial(update_kernel, group),
        out_shape=(jax.ShapeDtypeStruct(table.shape, jnp.float32),) * 2,
        in_specs=[pl.BlockSpec(memory_space=pltpu.VMEM)] * 3,
        out_specs=(pl.BlockSpec(memory_space=pltpu.VMEM),) * 2,
        scratch_shapes=[pltpu.VMEM(table.shape, jnp.float32)],
        cost_estimate=pl.CostEstimate(
            flops=6_000_000_000, bytes_accessed=5_000_000, transcendentals=0
        ),
        name="update_rows",
    )(recv, table, sums)


def swap(values, axis, bit):
    count = lax.axis_size(axis)
    return lax.ppermute(values, axis, [(i, i ^ (1 << bit)) for i in range(count)])


def scatter_sum(values, order):
    count = lax.axis_size("dp")
    bits = count.bit_length() - 1
    me = lax.axis_index("dp")
    left = list(range(bits))[::-1]
    values = values.reshape((2,) * bits + (values.shape[0] // count, values.shape[1]))
    for bit in order:
        axis = left.index(bit)
        mine = lax.rem(lax.div(me, 1 << bit), 2)
        sent = lax.dynamic_index_in_dim(values, 1 - mine, axis, keepdims=False)
        kept = lax.dynamic_index_in_dim(values, mine, axis, keepdims=False)
        values = kept + swap(sent, "dp", bit)
        left.remove(bit)
    return values


def body(hidden, out_grad, memory, w_key, w_value, row_owner, row_slot, mem_table, adagrad_sum):
    dp_count, tensor_count = lax.axis_size("dp"), lax.axis_size("tensor")
    owner_count = dp_count * tensor_count
    tokens = memory.shape[0]
    quarter = tokens // tensor_count
    features = w_key.shape[1] * tensor_count
    heads = row_owner.shape[1]
    scale_root = jnp.sqrt(jnp.asarray(features, jnp.float32))
    me = lax.axis_index("tensor")

    spread = tensor_count.bit_length() - 1
    firsts, extent = [], tokens
    for bit in range(spread):
        extent //= 2
        firsts.append(lax.rem(lax.div(me, 1 << bit), 2))
    first_row, extent = 0, tokens
    for mine in firsts:
        extent //= 2
        first_row = first_row + mine * extent
    owners = lax.dynamic_slice_in_dim(row_owner, first_row, quarter, 0).T
    slots = lax.dynamic_slice_in_dim(row_slot, first_row, quarter, 0).T.astype(jnp.float32)
    owner_ids = jnp.arange(owner_count, dtype=jnp.int32)
    hits = jnp.any(owners[None, :, :] == owner_ids[:, None, None], axis=1)
    token_ids = jnp.arange(quarter, dtype=jnp.int32)
    earlier = (token_ids[:, None] < token_ids[None, :]).astype(jnp.bfloat16)
    before = jnp.dot(hits.astype(jnp.bfloat16), earlier, preferred_element_type=jnp.float32)
    places = jnp.where(hits, before.astype(jnp.int32), -1)
    capacity = max(2, 2 * quarter * heads // owner_count)

    proj_key = jnp.dot(memory, w_key, preferred_element_type=jnp.float32)
    proj_value = jnp.dot(memory, w_value, preferred_element_type=jnp.float32)
    part_score = jnp.sum(hidden.astype(jnp.float32) * proj_key, axis=1)
    part_gate = jnp.sum(out_grad.astype(jnp.float32) * proj_value, axis=1)
    parts = jnp.stack([part_score, part_gate]).reshape(2, tokens // 128, 128)
    scores, gate_grad = sum_over_tensor(parts, tensor_count).reshape(2, tokens)
    gate_value = jax.nn.sigmoid(scores / scale_root)
    score_grad = gate_grad * gate_value * (1.0 - gate_value) / scale_root
    value_grad = (gate_value[:, None] * out_grad.astype(jnp.float32)).astype(jnp.bfloat16)
    key_grad = (score_grad[:, None] * hidden.astype(jnp.float32)).astype(jnp.bfloat16)
    hidden_grad = (score_grad[:, None] * proj_key).astype(jnp.bfloat16)

    def memory_grad_of(first, extent):
        value_part = lax.dynamic_slice_in_dim(value_grad, first, extent, 0)
        key_part = lax.dynamic_slice_in_dim(key_grad, first, extent, 0)
        return lax.dot_general(
            w_value, value_part, OVER_FEATURES, preferred_element_type=jnp.float32
        ) + lax.dot_general(w_key, key_part, OVER_FEATURES, preferred_element_type=jnp.float32)

    half = tokens // 2
    sent = memory_grad_of((1 - firsts[0]) * half, half)
    landed = swap(sent, "tensor", 0)
    memory_grad = memory_grad_of(firsts[0] * half, half) + landed
    for bit in range(1, spread):
        half //= 2
        sent = lax.dynamic_slice_in_dim(memory_grad, (1 - firsts[bit]) * half, half, 1)
        kept = lax.dynamic_slice_in_dim(memory_grad, firsts[bit] * half, half, 1)
        memory_grad = kept + swap(sent, "tensor", bit)

    over_tokens = (((0,), (0,)), ((), ()))
    key_total = lax.dot_general(memory, key_grad, over_tokens, preferred_element_type=jnp.float32)
    value_total = lax.dot_general(
        memory, value_grad, over_tokens, preferred_element_type=jnp.float32
    )
    order = list(range(dp_count.bit_length() - 1))
    other_order = order[1:2] + order[:1] + order[2:]
    key_weight_grad = scatter_sum(key_total, order)
    value_weight_grad = scatter_sum(value_total, other_order)

    packed = pack_rows(memory_grad, owners, slots, places, capacity)
    recv = exchange_rows(packed, dp_count, tensor_count)
    new_table, new_sum = update_rows(recv, mem_table, adagrad_sum)
    return (hidden_grad, key_weight_grad, value_weight_grad, new_table, new_sum)


def solution(mesh):
    return jax.shard_map(
        body,
        mesh=mesh,
        in_specs=(
            P("dp", "tensor"),
            P("dp", "tensor"),
            P("dp", None),
            P(None, "tensor"),
            P(None, "tensor"),
            P("dp", None),
            P("dp", None),
            P(("dp", "tensor"), None),
            P(("dp", "tensor"), None),
        ),
        out_specs=(
            P("dp", "tensor"),
            P("dp", "tensor"),
            P("dp", "tensor"),
            P(("dp", "tensor"), None),
            P(("dp", "tensor"), None),
        ),
        check_vma=False,
    )
```

time: 285 us -> 245 us (0.86)
  the two profiles are of different devices: /device:TPU:0 before, /device:TPU:15 now
where the time goes in v1:
time: 245 us; the launch traced here: 244 us
  Pallas kernels  96 us (39%)
  waiting for transfers between devices  68.7 us (28%)
  matrix products  29.4 us (12%)
  local copies, waits for them, and re-layouts  27.4 us (11%)
  other arithmetic  14.5 us (6%)
  starting transfers between devices  7.24 us (3%)
    pallas_call x1, Pallas kernels, exchange_rows(): pl.pallas_call(functools.partial(exchange_kernel, dp_count, tensor_count)...  75.1 us
    ppermute x8, waiting for transfers between devices, swap(): return lax.ppermute(values, axis, [(i, i ^ 1 << bit) for i in range(count)])  68.7 us
    unnamed x41, local copies, waits for them, and re-layouts  12.4 us
    pallas_call x1, Pallas kernels, pack_rows(): pl.pallas_call(functools.partial(pack_kernel, width), out_shape=jax.Shape...  8.7 us
    ppermute x8, starting transfers between devices, swap(): return lax.ppermute(values, axis, [(i, i ^ 1 << bit) for i in range(count)])  7.24 us
    pallas_call x1, Pallas kernels, update_rows(): pl.pallas_call(functools.partial(update_kernel, group), out_shape=(jax.Sh...  6.88 us
    dot_general x2, matrix products, memory_grad_of(): lax.dot_general(w_key, key_part, OVER_FEATURES, preferred_element_type=jn...  5.77 us
    squeeze x6, local copies, waits for them, and re-layouts, scatter_sum(): sent = lax.dynamic_index_in_dim(values, 1 - mine, axis, keepdims=False)  5.74 us
  transfers between devices with their start and end apart: 8, of which 5 were waited for; matrix products, arithmetic and copies ran while one was open for 17% of the time, Pallas kernels for 0%

profile of v1, /device:TPU:15, one launch (start us, length us, event | category | flops | bytes accessed | tf_op | source)
XLA Modules:
  0.0 244.1 jit_solution(14519025014714341260)
XLA Ops:
  0.7 2.6 %copy.42 = bf16[1024,640]{0,1:T(8,128)(2,1)} copy(bf16[1024,640]{1,0:T(8,128)(2,1)} %param.9) | data formatting | bytes 2621440 | tf_op args[0]
  3.2 2.4 %copy.43 = bf16[1024,640]{0,1:T(8,128)(2,1)} copy(bf16[1024,640]{1,0:T(8,128)(2,1)} %param.10) | data formatting | bytes 2621440 | tf_op args[1]
  5.7 5.4 %fusion.3 = (f32[1024]{0:T(1024)S(1)}, f32[1024,640]{0,1:T(8,128)}) fusion(bf16[1024,640]{0,1:T(8,128)(2,1)} %copy.42, bf16[1024,1280]{1,0:T(8,128)(2,1)S(1)} %copy-done, bf16[1280,640]{1,0:T(8,128)(2,1)} %param.12), kind=kOutput, calls=%fused_computation.11 | convolution fusion | flops 1679686656 | bytes 8196096 | tf_op jit(solution)/shard_map/dot_general | solution.py:265
  11.1 2.0 fusion.5
  13.6 5.3 %gate_sum.1 = f32[2,8,128]{2,1,0:T(8,128)} custom-call(f32[2,8,128]{2,1,0:T(8,128)} %pad_maximum_fusion.part_ref), custom_call_target="tpu_custom_call" | custom-call | tf_op jit(solution)/shard_map/gate_sum/pallas_call | solution.py:47
  20.3 2.7 %fusion.6 = bf16[1024,640]{0,1:T(8,128)(2,1)} fusion(bf16[1024,640]{0,1:T(8,128)(2,1)} %copy.43, f32[1024]{0:T(1024)S(1)} %divide_bitcast_fusion), kind=kLoop, calls=%fused_computation.14 | loop fusion | flops 1966080 | bytes 2625536 | tf_op jit(solution)/shard_map/convert_element_type | solution.py:273
  23.0 2.9 %fusion.9 = f32[512,1280]{0,1:T(8,128)S(1)} fusion(bf16[1280,640]{1,0:T(8,128)(2,1)} %param.13, bf16[1024,640]{0,1:T(8,128)(2,1)} %fusion.6, s32[]{:T(128)S(6)} %select_n.57), kind=kOutput, calls=%fused_computation.28 | convolution fusion | flops 838860800 | bytes 4915204 | tf_op jit(solution)/shard_map/dot_general | solution.py:280
  26.0 1.6 fusion.4
  27.6 2.7 %fusion.2 = f32[1280,512]{1,0:T(8,128)} fusion(f32[512,1280]{0,1:T(8,128)S(1)} %fusion.9, bf16[1280,640]{1,0:T(8,128)(2,1)S(1)} %copy-done.4, bf16[1024,640]{0,1:T(8,128)(2,1)S(1)} %get-tuple-element.24, s32[]{:T(128)S(6)} %select_n.57), kind=kOutput, calls=%fused_computation.10 | convolution fusion | flops 839516160 | bytes 7536644 | tf_op jit(solution)/shard_map/dot_general | solution.py:282
  30.7 4.9 %convolution_bitcast_fusion = f32[1280,640]{0,1:T(8,128)} fusion(bf16[1024,640]{0,1:T(8,128)(2,1)} %fusion.6, bf16[1024,1280]{1,0:T(8,128)(2,1)S(1)} %copy-done), kind=kOutput, calls=%fused_computation | convolution fusion | flops 1677721600 | bytes 7208960 | tf_op jit(solution)/shard_map/dot_general | solution.py:296
  35.7 4.6 %copy.45 = f32[1280,640]{1,0:T(8,128)} copy(f32[1280,640]{0,1:T(8,128)} %convolution_bitcast_fusion) | data formatting | bytes 6553600 | tf_op jit(solution)/shard_map/dot_general | solution.py:296
  40.2 2.7 %dynamic-slice_bitcast_fusion = f32[2,2,160,640]{3,2,1,0:T(8,128)} fusion(f32[2,2,2,160,640]{4,3,2,1,0:T(8,128)} %bitcast.65, s32[]{:T(128)S(6)} %select_n.53), kind=kLoop, calls=%fused_computation.18 | loop fusion | bytes 3276804 | tf_op jit(solution)/shard_map/jit(dynamic_index_in_dim)/squeeze | solution.py:229
  43.1 4.9 %convolution_bitcast_fusion.1 = f32[1280,640]{0,1:T(8,128)} fusion(bf16[1024,640]{0,1:T(8,128)(2,1)} %copy-done.6, bf16[1024,1280]{1,0:T(8,128)(2,1)S(1)} %copy-done), kind=kOutput, calls=%fused_computation.1 | convolution fusion | flops 1677721600 | bytes 7208960 | tf_op jit(solution)/shard_map/dot_general | solution.py:295
  48.0 4.6 %copy.44 = f32[1280,640]{1,0:T(8,128)} copy(f32[1280,640]{0,1:T(8,128)} %convolution_bitcast_fusion.1) | data formatting | bytes 6553600 | tf_op jit(solution)/shard_map/dot_general | solution.py:295
  52.6 2.8 %dynamic-slice_bitcast_fusion.1 = f32[2,2,160,640]{3,2,1,0:T(8,128)} fusion(f32[2,2,2,160,640]{4,3,2,1,0:T(8,128)} %bitcast.67, s32[]{:T(128)S(6)} %select_n.51), kind=kLoop, calls=%fused_computation.19 | loop fusion | bytes 3276804 | tf_op jit(solution)/shard_map/jit(dynamic_index_in_dim)/squeeze | solution.py:229
  57.7 1.4 copy.52
  60.5 2.8 %fusion.12 = f32[512,1280]{0,1:T(8,128)S(1)} fusion(bf16[1280,640]{1,0:T(8,128)(2,1)} %param.13, bf16[1024,640]{0,1:T(8,128)(2,1)S(1)} %copy-done.12, s32[]{:T(128)S(6)} %select_n.56), kind=kOutput, calls=%fused_computation.31 | convolution fusion | flops 838860800 | bytes 4915204 | tf_op jit(solution)/shard_map/dot_general | solution.py:280
  63.3 17.2 %collective-permute-done.3 = f32[2,2,160,640]{3,2,1,0:T(8,128)} collective-permute-done((f32[2,2,160,640]{3,2,1,0:T(8,128)}, f32[2,2,160,640]{3,2,1,0:T(8,128)}, u32[]{:S(2)}, u32[]{:S(2)}) %collective-permute-start.3) | collective-permute-done | bytes 1638432 | tf_op jit(solution)/shard_map/ppermute | solution.py:217
  80.5 1.8 bitcast_add_fusion
  82.7 9.9 %collective-permute-done = f32[2,2,160,640]{3,2,1,0:T(8,128)} collective-permute-done((f32[2,2,160,640]{3,2,1,0:T(8,128)}, f32[2,2,160,640]{3,2,1,0:T(8,128)}, u32[]{:S(2)}, u32[]{:S(2)}) %collective-permute-start) | collective-permute-done | bytes 1638432 | tf_op jit(solution)/shard_map/ppermute | solution.py:217
  92.7 1.8 bitcast_add_fusion.1
  95.9 3.1 %fusion.1 = f32[1280,512]{1,0:T(8,128)S(1)} fusion(f32[1280,512]{1,0:T(8,128)} %collective-permute-done.6, f32[512,1280]{0,1:T(8,128)S(1)} %fusion.12, bf16[1280,640]{1,0:T(8,128)(2,1)S(1)} %copy-done.5, bf16[1024,640]{0,1:T(8,128)(2,1)S(1)} %copy-done.7, s32[]{:T(128)S(6)} %select_n.56), kind=kOutput, calls=%fused_computation.9 | convolution fusion | flops 840171520 | bytes 10158084 | tf_op jit(solution)/shard_map/dot_general | solution.py:282
  99.5 10.7 %collective-permute-done.4 = f32[2,160,640]{2,1,0:T(8,128)S(1)} collective-permute-done((f32[2,160,640]{2,1,0:T(8,128)S(1)}, f32[2,160,640]{2,1,0:T(8,128)S(1)}, u32[]{:S(2)}, u32[]{:S(2)}) %collective-permute-start.4) | collective-permute-done | bytes 819232 | tf_op jit(solution)/shard_map/ppermute | solution.py:217
  110.3 2.4 collective-permute-start.5
  112.8 2.1 collective-permute-start.2
  115.6 22.8 %collective-permute-done.5 = f32[160,640]{1,0:T(8,128)S(1)} collective-permute-done((f32[160,640]{1,0:T(8,128)S(1)}, f32[160,640]{1,0:T(8,128)S(1)}, u32[]{:S(2)}, u32[]{:S(2)}) %collective-permute-start.5) | collective-permute-done | bytes 409632 | tf_op jit(solution)/shard_map/ppermute | solution.py:217
  139.3 8.0 %collective-permute-done.2 = f32[160,640]{1,0:T(8,128)S(1)} collective-permute-done((f32[160,640]{1,0:T(8,128)S(1)}, f32[160,640]{1,0:T(8,128)S(1)}, u32[]{:S(2)}, u32[]{:S(2)}) %collective-permute-start.2) | collective-permute-done | bytes 409632 | tf_op jit(solution)/shard_map/ppermute | solution.py:217
  149.5 8.7 %pack_rows.1.send_ref = f32[32,168,128]{2,1,0:T(8,128)} custom-call(f32[1280,256]{1,0:T(8,128)} %dynamic-slice_add_fusion.grads_ref, s32[8,256]{1,0:T(8,128)} %copy-done.15, f32[8,256]{1,0:T(8,128)} %get-tuple-element.28.slots_ref, s32[32,256]{1,0:T(8,128)} %fusion.7.places_ref), custom_call_target="tpu_custom_call" | custom-call | flops 6000000000 | bytes 4000000 | tf_op jit(solution)/shard_map/pack_rows/pallas_call | solution.py:158
  158.2 75.1 %exchange_rows.1.recv_ref = f32[32,168,128]{2,1,0:T(8,128)} custom-call(f32[32,168,128]{2,1,0:T(8,128)} %pack_rows.1.send_ref), custom_call_target="tpu_custom_call" | custom-call | flops 49999998976 | bytes 5505024 | tf_op jit(solution)/shard_map/exchange_rows/pallas_call | solution.py:106
  233.3 6.9 %update_rows.1 = (f32[512,160]{1,0:T(8,128)}, f32[512,160]{1,0:T(8,128)}) custom-call(f32[32,168,128]{2,1,0:T(8,128)} %exchange_rows.1.recv_ref, f32[512,160]{1,0:T(8,128)} %copy.50.table_ref, f32[512,160]{1,0:T(8,128)} %copy.51.sums_ref), custom_call_target="tpu_custom_call" | custom-call | flops 6000000000 | bytes 5000000 | tf_op jit(solution)/shard_map/update_rows/pallas_call | solution.py:202
  240.2 1.9 copy.53
  242.1 1.9 copy.54
  (61 shorter events, 12.6 us)
Async XLA Ops:
  0.6 5.1 %copy-start = (bf16[1024,1280]{1,0:T(8,128)(2,1)S(1)}, bf16[1024,1280]{1,0:T(8,128)(2,1)}, u32[]{:S(2)}) copy-start(bf16[1024,1280]{1,0:T(8,128)(2,1)} %param.11) | copy-start | bytes 7864324
  5.7 5.4 %copy-start.8 = (bf16[1024,640]{0,1:T(8,128)(2,1)S(1)}, bf16[1024,640]{0,1:T(8,128)(2,1)}, u32[]{:S(2)}) copy-start(bf16[1024,640]{0,1:T(8,128)(2,1)} %copy.43) | copy-start | bytes 3932164
  5.7 5.4 %copy-start.16 = (bf16[1280,640]{1,0:T(8,128)(2,1)S(1)}, bf16[1280,640]{1,0:T(8,128)(2,1)}, u32[]{:S(2)}) copy-start(bf16[1280,640]{1,0:T(8,128)(2,1)} %param.13) | copy-start | bytes 4915204
  23.0 2.9 %copy-start.10 = (bf16[1024,640]{0,1:T(8,128)(2,1)S(1)}, bf16[1024,640]{0,1:T(8,128)(2,1)}, u32[]{:S(2)}) copy-start(bf16[1024,640]{0,1:T(8,128)(2,1)} %copy.42) | copy-start | bytes 3932164
  23.0 2.9 %copy-start.11 = (f32[1024,640]{0,1:T(8,128)S(1)}, f32[1024,640]{0,1:T(8,128)}, u32[]{:S(2)}) copy-start(f32[1024,640]{0,1:T(8,128)} %get-tuple-element.27) | copy-start | bytes 7864324
  26.0 1.7 copy-start.4
  27.6 2.7 %copy-start.6 = (bf16[1024,640]{0,1:T(8,128)(2,1)}, bf16[1024,640]{0,1:T(8,128)(2,1)S(1)}, u32[]{:S(2)}) copy-start(bf16[1024,640]{0,1:T(8,128)(2,1)S(1)} %get-tuple-element.24) | copy-start | bytes 3932164
  30.3 65.6 %collective-permute-start.6 = (f32[1280,512]{1,0:T(8,128)}, f32[1280,512]{1,0:T(8,128)}, u32[]{:S(2)}, u32[]{:S(2)}) collective-permute-start(f32[1280,512]{1,0:T(8,128)} %fusion.2), channel_id=1, source_target_pairs={{0,1},{1,0},{2,3},{3,2},{4,5},{5,4},{6,7},{7,6},{8,9},{9,8},{10,11... | collective-permute-start | bytes 7864328 | tf_op jit(solution)/shard_map/ppermute | solution.py:217
  43.0 37.6 %collective-permute-start.3 = (f32[2,2,160,640]{3,2,1,0:T(8,128)}, f32[2,2,160,640]{3,2,1,0:T(8,128)}, u32[]{:S(2)}, u32[]{:S(2)}) collective-permute-start(f32[2,2,160,640]{3,2,1,0:T(8,128)} %dynamic-slice_bitcast_fusion), channel_id=1, source_target_pairs={{0,8},{4,12},{8,0},{12,4},{16,24},{20,28},{24,16},{28,20},{1,9},{5... | collective-permute-start | bytes 4915208 | tf_op jit(solution)/shard_map/ppermute | solution.py:217
  52.6 3.1 %copy-start.13 = (f32[512,160]{0,1:T(8,128)S(1)}, f32[512,160]{0,1:T(8,128)}, u32[]{:S(2)}) copy-start(f32[512,160]{0,1:T(8,128)} %param.16) | copy-start | bytes 983044
  52.6 4.1 %copy-start.14 = (f32[512,160]{0,1:T(8,128)S(1)}, f32[512,160]{0,1:T(8,128)}, u32[]{:S(2)}) copy-start(f32[512,160]{0,1:T(8,128)} %param.17) | copy-start | bytes 983044
  55.4 2.3 copy-start.9
  55.4 37.3 %collective-permute-start = (f32[2,2,160,640]{3,2,1,0:T(8,128)}, f32[2,2,160,640]{3,2,1,0:T(8,128)}, u32[]{:S(2)}, u32[]{:S(2)}) collective-permute-start(f32[2,2,160,640]{3,2,1,0:T(8,128)} %dynamic-slice_bitcast_fusion.1), channel_id=1, source_target_pairs={{0,4},{4,0},{8,12},{12,8},{16,20},{20,16},{24,28},{28,24},{1,5},{5... | collective-permute-start | bytes 4915208 | tf_op jit(solution)/shard_map/ppermute | solution.py:217
  56.7 3.8 %copy-start.12 = (bf16[1024,640]{0,1:T(8,128)(2,1)S(1)}, bf16[1024,640]{0,1:T(8,128)(2,1)}, u32[]{:S(2)}) copy-start(bf16[1024,640]{0,1:T(8,128)(2,1)} %fusion.6) | copy-start | bytes 3932164
  60.4 2.9 %copy-start.15 = (s32[8,256]{1,0:T(8,128)}, s32[8,256]{1,0:T(8,128)S(1)}, u32[]{:S(2)}) copy-start(s32[8,256]{1,0:T(8,128)S(1)} %get-tuple-element.29.owners_ref) | copy-start | bytes 24580
  60.5 20.0 %copy-start.2 = (f32[1280,640]{1,0:T(8,128)S(1)}, f32[1280,640]{1,0:T(8,128)}, u32[]{:S(2)}) copy-start(f32[1280,640]{1,0:T(8,128)} %copy.45) | copy-start | bytes 9830404
  80.5 12.2 %copy-start.3 = (f32[1280,640]{1,0:T(8,128)S(1)}, f32[1280,640]{1,0:T(8,128)}, u32[]{:S(2)}) copy-start(f32[1280,640]{1,0:T(8,128)} %copy.44) | copy-start | bytes 9830404
  82.4 27.7 %collective-permute-start.4 = (f32[2,160,640]{2,1,0:T(8,128)S(1)}, f32[2,160,640]{2,1,0:T(8,128)S(1)}, u32[]{:S(2)}, u32[]{:S(2)}) collective-permute-start(f32[2,160,640]{2,1,0:T(8,128)S(1)} %dynamic-slice_bitcast_fusion.2), channel_id=1, source_target_pairs={{0,4},{4,0},{8,12},{12,8},{16,20},{20,16},{24,28},{28,24},{1,5},{5... | collective-permute-start | bytes 2457608 | tf_op jit(solution)/shard_map/ppermute | solution.py:217
  92.7 3.2 %copy-start.7 = (bf16[1024,640]{0,1:T(8,128)(2,1)S(1)}, bf16[1024,640]{0,1:T(8,128)(2,1)}, u32[]{:S(2)}) copy-start(bf16[1024,640]{0,1:T(8,128)(2,1)} %copy-done.6) | copy-start | bytes 3932164
  94.5 1.5 copy-start.5
  94.6 18.1 %collective-permute-start.1 = (f32[2,160,640]{2,1,0:T(8,128)S(1)}, f32[2,160,640]{2,1,0:T(8,128)S(1)}, u32[]{:S(2)}, u32[]{:S(2)}) collective-permute-start(f32[2,160,640]{2,1,0:T(8,128)S(1)} %dynamic-slice_bitcast_fusion.3), channel_id=1, source_target_pairs={{0,8},{4,12},{8,0},{12,4},{16,24},{20,28},{24,16},{28,20},{1,9},{5... | collective-permute-start | bytes 2457608 | tf_op jit(solution)/shard_map/ppermute | solution.py:217
  99.2 48.9 %collective-permute-start.7 = (f32[1280,256]{1,0:T(8,128)S(1)}, f32[1280,256]{1,0:T(8,128)S(1)}, u32[]{:S(2)}, u32[]{:S(2)}) collective-permute-start(f32[1280,256]{1,0:T(8,128)S(1)} %constant_dynamic-slice_fusion), channel_id=1, source_target_pairs={{0,2},{1,3},{2,0},{3,1},{4,6},{5,7},{6,4},{7,5},{8,10},{9,11},{10,... | collective-permute-start | bytes 3932168 | tf_op jit(solution)/shard_map/ppermute | solution.py:217
  110.3 28.2 %collective-permute-start.5 = (f32[160,640]{1,0:T(8,128)S(1)}, f32[160,640]{1,0:T(8,128)S(1)}, u32[]{:S(2)}, u32[]{:S(2)}) collective-permute-start(f32[160,640]{1,0:T(8,128)S(1)} %dynamic-slice_bitcast_fusion.4), channel_id=1, source_target_pairs={{0,16},{4,20},{8,24},{12,28},{16,0},{20,4},{24,8},{28,12},{1,17},{... | collective-permute-start | bytes 1228808 | tf_op jit(solution)/shard_map/ppermute | solution.py:217
  112.8 34.5 %collective-permute-start.2 = (f32[160,640]{1,0:T(8,128)S(1)}, f32[160,640]{1,0:T(8,128)S(1)}, u32[]{:S(2)}, u32[]{:S(2)}) collective-permute-start(f32[160,640]{1,0:T(8,128)S(1)} %dynamic-slice_bitcast_fusion.5), channel_id=1, source_target_pairs={{0,16},{4,20},{8,24},{12,28},{16,0},{20,4},{24,8},{28,12},{1,17},{... | collective-permute-start | bytes 1228808 | tf_op jit(solution)/shard_map/ppermute | solution.py:217
  233.3 10.8 %copy-start.1 = (bf16[1024,1280]{1,0:T(8,128)(2,1)S(1)}, bf16[1024,1280]{1,0:T(8,128)(2,1)}, u32[]{:S(2)}) copy-start(bf16[1024,1280]{1,0:T(8,128)(2,1)} %param.11) | copy-start | bytes 7864324
